TPU v7x, 128 devices: a whole 4x4x4 slice. The times are simulated.
128 devices in a mesh: pole: 8 (over x, z_lo), blk: 16 (over y, z_hi, core).
Axes of the slice: x: 4, y: 4, z: 4 (z_hi: 2, z_lo: 2; z = z_hi * 2 + z_lo), core: 2. Of those that a mesh axis runs over, the one named last changes fastest.
Arguments:
- inverse_block: float32 [8, 2, 4096, 4096], P('pole', None, 'blk'), may hold values from -0.09375 to 0.09375
- factor: float32 [8, 4096, 2, 512], P('pole', 'blk'), may hold values from -0.75 to 0.75
- diag_inverse: float32 [8, 2, 2, 256, 256], P('pole', None, None, 'blk'), may hold values from -6 to 6
- pole_weight: float32 [8, 2], P('pole'), may hold values from -4 to 4
- block_ids: int32 [128, 8], P(('pole', 'blk')), may hold values from 0 to 31, as said below
- block_count: int32 [128], P(('pole', 'blk')), may hold values from 1 to 8, 576 in all
- basis: float32 [128, 2048, 1024], P(('pole', 'blk')), may hold values from -0.1875 to 0.1875
- column_basis: float32 [128, 2048, 512], P(('pole', 'blk')), may hold values from -0.25 to 0.25
Outputs:
- diag_density: float32 [2, 256, 256], P(None, 'blk')
- density: float32 [128, 2048], P(('pole', 'blk'))
Inputs may be any that keep to these rules, and one draw needn't show every extreme that they name: Entries of block_ids beyond a batch's block_count are not read; block_count reaches 8 in every draw. With b = g mod 16, every entry of block_ids[g] names a block of rows b' * 4096 // 16 to (b' + 1) * 4096 // 16 for some b' between b - 2 and b + 2.
All inputs are finite; a program needn't handle non-finite values. No bound on the sum of `block_count` on one device may be relied on, other than what follows from the above.
Results may differ from a plain program's by a relative error of at most 0.0003.
Values sent between devices are 32-bit elements; how exact they have to be, the bound alone decides.
A program may use at most 128 MiB of HBM per device.

v0:
```python
import jax
import jax.numpy as jnp
from jax import lax
from jax.experimental import pallas as pl
from jax.experimental.pallas import tpu as pltpu
from jax.sharding import PartitionSpec as P

MESH = pl.DeviceIdType.MESH
F32 = jnp.float32
BF16 = jnp.bfloat16
CH = 4
REACH = 2


def split(x):
    high = x.astype(BF16)
    return high, (x - high.astype(F32)).astype(BF16)


def dot(a, b):
    return jnp.dot(a, b, preferred_element_type=F32)


def dot3(ah, al, bh, bl):
    return dot(ah, bh) + dot(ah, bl) + dot(al, bh)


def kernel(
    w_ref, ids_ref, cnt_ref, g_ref, l_ref, d_ref, basis_ref, cb_ref,
    diag_ref, dens_ref,
    lbuf, gh, gl, stage, bh, bl, cbuf, mbuf, ybuf, rsb, sb, zb, dpart, dgb, dpb, dsum,
    acc, dacc, selh, lth, ltl, dv, mloc,
    ag_s, ag_r, co_s, co_r, rs_s, rs_r, zl_s, zl_r, re_s, re_r, ax_s, ax_r,
    dg_s, dg_r, dp_s, dp_r, st_sem, loc_sem, cb_sem,
):
    p = lax.axis_index("pole")
    b = lax.axis_index("blk")
    x, zl = p // 2, lax.rem(p, 2)
    y, zh, co = b // 4, lax.rem(b // 2, 2), lax.rem(b, 2)
    oz, oc = 1 - zh, 1 - co
    yu, yd, yo = lax.rem(y + 1, 4), lax.rem(y + 3, 4), lax.rem(y + 2, 4)

    def at(yy, zz, cc):
        return yy * 4 + zz * 2 + cc

    up, down, over, sib = (p, at(yu, zh, co)), (p, at(yd, zh, co)), (p, at(y, oz, co)), (p, at(y, zh, oc))

    own = [pltpu.make_async_copy(l_ref.at[c], lbuf.at[c, b], loc_sem.at[c]) for c in range(CH)]
    for cp in own:
        cp.start()
    dcopy = pltpu.make_async_copy(d_ref, dv, loc_sem.at[CH])
    dcopy.start()

    def g_copy(i):
        return pltpu.make_async_copy(
            g_ref.at[i // 16, :, pl.ds(pl.multiple_of(lax.rem(i, 16) * 256, 256), 256)], stage.at[i], st_sem.at[i])

    def b_copy(i):
        return pltpu.make_async_copy(
            basis_ref.at[pl.ds(pl.multiple_of((i // 4) * 256, 256), 256),
                         pl.ds(pl.multiple_of(lax.rem(i, 4) * 256, 256), 256)], stage.at[i], st_sem.at[i])

    @pl.loop(0, 32)
    def _(i):
        g_copy(i).start()

    bar = pltpu.get_barrier_semaphore()

    @pl.loop(1, 16)
    def _(d):
        pl.semaphore_signal(bar, inc=1, device_id=(p, lax.rem(b + d, 16)), device_id_type=MESH)

    @pl.loop(1, 8)
    def _(d):
        pl.semaphore_signal(bar, inc=1, device_id=(lax.rem(p + d, 8), b), device_id_type=MESH)

    for cp in own:
        cp.wait()
    pl.semaphore_wait(bar, 22)

    def rc(src, dst, s, r, dev):
        return pltpu.make_async_remote_copy(src, dst, s, r, device_id=dev, device_id_type=MESH)

    def ag(c, kind, slot, dev, rows=None):
        ref = lbuf.at[c, slot] if rows is None else lbuf.at[c, slot, pl.ds(rows, 128)]
        return rc(ref, ref, ag_s.at[c, kind], ag_r.at[c, kind], dev)

    def cf(c, i, slot):
        ref = lbuf.at[c, slot]
        return rc(ref, ref, co_s.at[c, i], co_r.at[c, i], sib)

    def slot_of(i, cc):
        return at(lax.rem(y + lax.rem(i, 4), 4), lax.rem(zh + i // 4, 2), cc)

    def send_own(c):
        ag(c, 0, b, up).start()
        ag(c, 1, b, down).start()
        ag(c, 2, b, over).start()
        cf(c, 0, b).start()

    s1, s2, s3, s4 = at(yd, zh, co), at(yu, zh, co), at(y, oz, co), at(yo, zh, co)
    s5, s6, s7 = at(yd, oz, co), at(yu, oz, co), at(yo, oz, co)

    def early(c, ahead):
        ag(c, 0, s1, up).wait_recv()
        ag(c, 3, s1, up, 0).start()
        cf(c, 3, s1).start()
        ag(c, 1, s2, down).wait_recv()
        ag(c, 4, s2, down, 128).start()
        cf(c, 1, s2).start()
        ag(c, 2, s3, over).wait_recv()
        ag(c, 5, s3, up).start()
        ag(c, 6, s3, down).start()
        cf(c, 4, s3).start()
        ahead()

    def middle(c):
        ag(c, 3, s4, up, 0).wait_recv()
        ag(c, 7, s4, over, 0).start()
        ag(c, 4, s4, down, 128).wait_recv()
        ag(c, 8, s4, over, 128).start()
        cf(c, 2, s4).start()

    def late(c):
        ag(c, 5, s5, up).wait_recv()
        cf(c, 7, s5).start()
        ag(c, 6, s6, down).wait_recv()
        cf(c, 5, s6).start()
        ag(c, 7, s7, over, 0).wait_recv()
        ag(c, 8, s7, over, 128).wait_recv()
        cf(c, 6, s7).start()

    def piece(c, slot):
        v = lbuf[c, slot]
        h, l = split(v)
        h2 = jnp.concatenate([-h[:, 128:], h[:, :128]], axis=1)
        l2 = jnp.concatenate([-l[:, 128:], l[:, :128]], axis=1)
        return dot3(gh[slot], gl[slot], h, l) + dot3(gh[16 + slot], gl[16 + slot], h2, l2)

    def products(c, low, high):
        @pl.loop(low, high)
        def _(i):
            acc[...] += piece(c, slot_of(i, co))
            o = slot_of(i, oc)
            cf(c, i, o).wait_recv()
            acc[...] += piece(c, o)

    wr, wi = w_ref[0, 0], w_ref[0, 1]

    def t1(c):
        a = acc[...]
        ar, ai = a[:, :128], a[:, 128:]
        yr, yi = wi * ai - wr * ar, -(wr * ai + wi * ar)
        ybuf[c] = yr
        for d in range(1, 4):
            xx = lax.rem(x + d, 4)
            rc(ybuf.at[c, pl.ds(pl.multiple_of(xx * 64, 64), 64)], rsb.at[c, d], rs_s.at[c, d], rs_r.at[c, d],
               (xx * 2 + zl, b)).start()
        yrh, yrl = split(yr)
        yih, yil = split(yi)
        j = 2 * (c // 2)
        for h in range(2):
            th, tl = lth[j + h], ltl[j + h]
            dpart[c, pl.ds(h * 128, 128)] = dot3(th[:128], tl[:128], yrh, yrl) - dot3(th[128:], tl[128:], yih, yil)

    def t1b(c):
        tot = ybuf[c, pl.ds(pl.multiple_of(x * 64, 64), 64)]
        for d in range(1, 4):
            rc(rsb.at[c, d], rsb.at[c, d], rs_s.at[c, d], rs_r.at[c, d], sib).wait_recv()
            tot = tot + rsb[c, d]
        sb[c] = tot
        rc(sb.at[c], zb.at[c], zl_s.at[c], zl_r.at[c], (x * 2 + 1 - zl, b)).start()

    def t2(c):
        rc(sb.at[c], zb.at[c], zl_s.at[c], zl_r.at[c], sib).wait_recv()
        mbuf[c, REACH, x] = sb[c] + zb[c]
        for off in (2, -2, 1, -1):
            k = REACH - off
            rc(mbuf.at[c, REACH, x], mbuf.at[c, k, x], re_s.at[c, k], re_r.at[c, k],
               (p, lax.rem(b + 16 + off, 16))).start()

    def t3(c):
        for k in (0, 1, 3, 4):
            rc(mbuf.at[c, k, x], mbuf.at[c, k, x], re_s.at[c, k], re_r.at[c, k], sib).wait_recv()
        for d in range(1, 4):
            rc(mbuf.at[c, :, x], mbuf.at[c, :, x], ax_s.at[c, d], ax_r.at[c, d],
               (lax.rem(x + d, 4) * 2 + zl, b)).start()

    def t4(c):
        for d in range(1, 4):
            xx = lax.rem(x + 4 - d, 4)
            rc(mbuf.at[c, :, xx], mbuf.at[c, :, xx], ax_s.at[c, d], ax_r.at[c, d], sib).wait_recv()
        for k in range(2 * REACH + 1):
            for q in range(4):
                mloc[k * 4 + q] = mbuf[c, k, q]
        count = cnt_ref[0]
        first = (b - REACH) * 2

        @pl.loop(0, 8)
        def _(s):
            n = jnp.clip(ids_ref[0, s] - first, 0, 4 * REACH + 1)
            keep = jnp.where(s < count, 1.0, 0.0).astype(F32)
            for i in range(2):
                h, l = split(mloc[n * 2 + i] * keep)
                rows = pl.ds(pl.multiple_of(s * 128 + i * 64, 64), 64)
                selh[rows, :128] = h
                selh[rows, 128:] = l

        @pl.loop(0, 8)
        def _(r):
            pq = dot(bh[r], selh[...])
            q = dot(bl[r], selh[:, :128])
            rows = pl.ds(pl.multiple_of(r * 256, 256), 256)
            dacc[rows] += (pq[:, :128] + pq[:, 128:] + q) * cbuf[c, rows]

    send_own(0)
    send_own(1)

    @pl.loop(0, 32)
    def _(i):
        g_copy(i).wait()
        h, l = split(stage[i])
        gh[i] = h
        gl[i] = l
        b_copy(i).start()

    for c in range(CH):
        pltpu.make_async_copy(cb_ref.at[:, pl.ds(c * 128, 128)], cbuf.at[c], cb_sem.at[c]).start()

    @pl.loop(0, CH)
    def _(c):
        h, l = split(lbuf[c, b].T)
        lth[c] = h
        ltl[c] = l

    early(0, lambda: send_own(2))

    @pl.loop(0, 32)
    def _(i):
        b_copy(i).wait()
        h, l = split(stage[i])
        bh[i // 4, :, pl.ds(pl.multiple_of(lax.rem(i, 4) * 256, 256), 256)] = h
        bl[i // 4, :, pl.ds(pl.multiple_of(lax.rem(i, 4) * 256, 256), 256)] = l

    for c in range(CH):
        pltpu.make_async_copy(cb_ref.at[:, pl.ds(c * 128, 128)], cbuf.at[c], cb_sem.at[c]).wait()
    dcopy.wait()
    dacc[...] = jnp.zeros_like(dacc)

    @pl.loop(0, CH)
    def _(c):
        @pl.when(c < CH - 1)
        def _():
            def ahead():
                @pl.when(c + 3 < CH)
                def _():
                    send_own(c + 3)

            early(c + 1, ahead)

        @pl.when(c > 0)
        def _():
            t1b(c - 1)

        middle(c)
        acc[...] = jnp.zeros_like(acc)
        products(c, 0, 5)

        @pl.when(c > 0)
        def _():
            t2(c - 1)

        late(c)
        products(c, 5, 8)
        t1(c)

        @pl.when(c > 0)
        def _():
            t3(c - 1)
            t4(c - 1)

    last = CH - 1
    t1b(last)
    t2(last)

    def dg(d, row):
        return rc(dpart.at[:, pl.ds(pl.multiple_of(row * 16, 16), 16)], dgb.at[d], dg_s.at[d], dg_r.at[d],
                  (p, lax.rem(b + d, 16)))

    @pl.loop(1, 16)
    def _(d):
        dg(d, lax.rem(b + d, 16)).start()

    t3(last)

    dsum[...] = dpart[:, pl.ds(pl.multiple_of(b * 16, 16), 16)]

    @pl.loop(1, 16)
    def _(d):
        dg(d, 0).wait_recv()
        dsum[...] += dgb[d]

    for c in range(CH):
        cols = slice((c % 2) * 128, (c % 2) * 128 + 128)
        dsum[c] = wr * dv[0, c // 2, :, cols] - wi * dv[1, c // 2, :, cols] - dsum[c]

    def dp(d):
        return rc(dsum, dpb.at[d], dp_s.at[d], dp_r.at[d], (lax.rem(p + d, 8), b))

    @pl.loop(1, 8)
    def _(d):
        dp(d).start()

    t4(last)

    for r in range(16):
        dens_ref[r, :] = jnp.sum(dacc[r * 128 : (r + 1) * 128].T, axis=0)

    dpb[0] = dsum[...]

    @pl.loop(1, 8)
    def _(d):
        dp(d).wait_recv()
        dpb[0] += dpb[d]

    for c in range(CH):
        diag_ref[c // 2, :, (c % 2) * 128 : (c % 2) * 128 + 128] = dpb[0, c]

    @pl.loop(0, CH)
    def _(c):
        for kind in range(9):
            rows = {3: 0, 4: 128, 7: 0, 8: 128}.get(kind)
            ag(c, kind, b, sib, rows).wait_send()
        for i in range(8):
            cf(c, i, b).wait_send()
        for d in range(1, 4):
            rc(rsb.at[c, d], rsb.at[c, d], rs_s.at[c, d], rs_r.at[c, d], sib).wait_send()
            rc(mbuf.at[c, :, x], mbuf.at[c, :, x], ax_s.at[c, d], ax_r.at[c, d], sib).wait_send()
        rc(sb.at[c], zb.at[c], zl_s.at[c], zl_r.at[c], sib).wait_send()
        for k in (0, 1, 3, 4):
            rc(mbuf.at[c, k, x], mbuf.at[c, k, x], re_s.at[c, k], re_r.at[c, k], sib).wait_send()

    @pl.loop(1, 16)
    def _(d):
        dg(d, 0).wait_send()

    @pl.loop(1, 8)
    def _(d):
        dp(d).wait_send()


def body(inverse_block, factor, diag_inverse, pole_weight, block_ids, block_count, basis, column_basis):
    panels = factor[0].reshape(256, 2, CH, 128).transpose(2, 0, 1, 3).reshape(CH, 256, 256)
    dma = pltpu.SemaphoreType.DMA
    anyspace = pl.BlockSpec(memory_space=pl.ANY)
    smem = pl.BlockSpec(memory_space=pltpu.SMEM)
    vmem = pl.BlockSpec(memory_space=pltpu.VMEM)
    diag, dens = pl.pallas_call(
        kernel,
        name="selinv",
        out_shape=(jax.ShapeDtypeStruct((2, 16, 256), F32), jax.ShapeDtypeStruct((16, 128), F32)),
        in_specs=[smem, smem, smem, anyspace, anyspace, anyspace, anyspace, anyspace],
        out_specs=(vmem, vmem),
        scratch_shapes=[
            pltpu.VMEM((CH, 16, 256, 256), F32),
            pltpu.VMEM((32, 256, 256), BF16),
            pltpu.VMEM((32, 256, 256), BF16),
            pltpu.VMEM((32, 256, 256), F32),
            pltpu.VMEM((8, 256, 1024), BF16),
            pltpu.VMEM((8, 256, 1024), BF16),
            pltpu.VMEM((CH, 2048, 128), F32),
            pltpu.VMEM((CH, 5, 4, 64, 128), F32),
            pltpu.VMEM((CH, 256, 128), F32),
            pltpu.VMEM((CH, 4, 64, 128), F32),
            pltpu.VMEM((CH, 64, 128), F32),
            pltpu.VMEM((CH, 64, 128), F32),
            pltpu.VMEM((CH, 256, 128), F32),
            pltpu.VMEM((16, CH, 16, 128), F32),
            pltpu.VMEM((8, CH, 16, 128), F32),
            pltpu.VMEM((CH, 16, 128), F32),
            pltpu.VMEM((256, 256), F32),
            pltpu.VMEM((2048, 128), F32),
            pltpu.VMEM((1024, 256), BF16),
            pltpu.VMEM((CH, 256, 256), BF16),
            pltpu.VMEM((CH, 256, 256), BF16),
            pltpu.VMEM((2, 2, 16, 256), F32),
            pltpu.VMEM((20, 64, 128), F32),
            dma((CH, 9)), dma((CH, 9)), dma((CH, 8)), dma((CH, 8)),
            dma((CH, 4)), dma((CH, 4)), dma((CH,)), dma((CH,)), dma((CH, 5)), dma((CH, 5)), dma((CH, 4)), dma((CH, 4)),
            dma((16,)), dma((16,)), dma((8,)), dma((8,)), dma((32,)), dma((CH + 1,)), dma((CH,)),
        ],
        compiler_params=pltpu.CompilerParams(
            collective_id=0, has_side_effects=True, vmem_limit_bytes=67_000_000),
    )(pole_weight, block_ids, block_count,
      inverse_block[0], panels, diag_inverse[0], basis[0], column_basis[0])
    return diag, dens.reshape(1, 2048)


def solution(mesh):
    in_specs = (
        P("pole", None, "blk", None),
        P("pole", "blk", None, None),
        P("pole", None, None, "blk", None),
        P("pole", None),
        P(("pole", "blk"), None),
        P(("pole", "blk")),
        P(("pole", "blk"), None, None),
        P(("pole", "blk"), None, None),
    )
    out_specs = (P(None, "blk", None), P(("pole", "blk"), None))
    return jax.shard_map(body, mesh=mesh, in_specs=in_specs, out_specs=out_specs, check_vma=False)
```

profile of v0, /device:TPU:0, one launch (start us, length us, event | category | flops | bytes accessed | tf_op | source)
XLA Modules:
  0.0 167.4 jit_solution(16827380648359453645)
XLA Ops:
  0.6 2.2 %reshape_squeeze.3 = f32[256,2,4,128]{3,2,1,0:T(4,128)S(1)} reshape(f32[1,256,2,512]{3,2,1,0:T(2,128)} %param.9) | data formatting | bytes 2097152 | tf_op jit(solution)/shard_map/reshape;squeeze | solution.py:353
  2.9 0.5 copy.12
  3.4 1.8 %reshape.10.l_ref = f32[4,256,256]{2,1,0:T(8,128)} reshape(f32[4,256,2,128]{3,2,1,0:T(2,128)S(1)} %bitcast.11) | data formatting | bytes 2097152 | tf_op jit(solution)/shard_map/reshape | solution.py:353
  5.9 158.8 %selinv.1 = (f32[2,16,256]{2,1,0:T(8,128)}, f32[16,128]{1,0:T(8,128)}) custom-call(f32[1,2]{1,0:T(1,128)} %w_ref.1, s32[1,8]{1,0:T(1,128)} %ids_ref.1, s32[1]{0:T(128)S(6)} %copy.15.cnt_ref, f32[2,256,4096]{2,1,0:T(8,128)} %bitcast.8, f32[4,256,256]{2,1,0:T(8,128)} %reshape.10.l_ref, f32[2,2,16,256]{3,2,1,0:T(8,128)} %bitcast.12, f32[2048,1024]{1,0:T(8,128)} %bitcast.9, ...), custom_call_target="tpu_custom_call" | custom-call | tf_op jit(solution)/shard_map/selinv/pallas_call | solution.py:358
  164.7 1.4 copy.16
  166.1 1.3 copy.17
where the time goes:
time: 168 us; the launch traced here: 167 us
  Pallas kernels  159 us (95%)
  local copies, waits for them, and re-layouts  7.28 us (4%)
    pallas_call x1, Pallas kernels, body(): pl.pallas_call(kernel, name='selinv', out_shape=(jax.ShapeDtypeStruct((2,...  159 us

commit v1 on v0

--- a/solution.py
+++ b/solution.py
@@ -12,6 +12,22 @@
 REACH = 2
 
 
+ORDER = (
+    "E0Z0C0Y2V2E1Z1F0",
+    "P0Y3H0Q0V3F1E2Z2",
+    "P110H1Q1F2E3Z3P2",
+    "2011H2Q230F3P321",
+    "H3Q312B031132240",
+    "23B1D03233S041B2",
+    "42B343",
+)
+
+
+def events():
+    text = "".join(ORDER)
+    return [(text[i], int(text[i + 1])) for i in range(0, len(text), 2)]
+
+
 def split(x):
     high = x.astype(BF16)
     return high, (x - high.astype(F32)).astype(BF16)
@@ -30,8 +46,8 @@
     diag_ref, dens_ref,
     lbuf, gh, gl, stage, bh, bl, cbuf, mbuf, ybuf, rsb, sb, zb, dpart, dgb, dpb, dsum,
     acc, dacc, selh, lth, ltl, dv, mloc,
-    ag_s, ag_r, co_s, co_r, rs_s, rs_r, zl_s, zl_r, re_s, re_r, ax_s, ax_r,
-    dg_s, dg_r, dp_s, dp_r, st_sem, loc_sem, cb_sem,
+    ag_s, ag_r, co_s, co_r, rs_s, rs_r, zl_s, zl_r, re_s, re_r, ax_s, ax_r, sx_s, sx_r,
+    dg_s, dg_r, dp_s, dp_r, st_sem, own_sem, loc_sem, cb_sem,
 ):
     p = lax.axis_index("pole")
     b = lax.axis_index("blk")
@@ -45,10 +61,14 @@
 
     up, down, over, sib = (p, at(yu, zh, co)), (p, at(yd, zh, co)), (p, at(y, oz, co)), (p, at(y, zh, oc))
 
-    own = [pltpu.make_async_copy(l_ref.at[c], lbuf.at[c, b], loc_sem.at[c]) for c in range(CH)]
+    own = [
+        pltpu.make_async_copy(
+            l_ref.at[:, k, pl.ds(c * 128, 128)], lbuf.at[c, b, :, pl.ds(k * 128, 128)], own_sem.at[c, k])
+        for c in range(CH) for k in range(2)
+    ]
     for cp in own:
         cp.start()
-    dcopy = pltpu.make_async_copy(d_ref, dv, loc_sem.at[CH])
+    dcopy = pltpu.make_async_copy(d_ref, dv, loc_sem.at[0])
     dcopy.start()
 
     def g_copy(i):
@@ -74,9 +94,9 @@
     def _(d):
         pl.semaphore_signal(bar, inc=1, device_id=(lax.rem(p + d, 8), b), device_id_type=MESH)
 
+    pl.semaphore_wait(bar, 22)
     for cp in own:
         cp.wait()
-    pl.semaphore_wait(bar, 22)
 
     def rc(src, dst, s, r, dev):
         return pltpu.make_async_remote_copy(src, dst, s, r, device_id=dev, device_id_type=MESH)
@@ -92,29 +112,32 @@
     def slot_of(i, cc):
         return at(lax.rem(y + lax.rem(i, 4), 4), lax.rem(zh + i // 4, 2), cc)
 
-    def send_own(c):
+    def own_y(c):
         ag(c, 0, b, up).start()
         ag(c, 1, b, down).start()
+        cf(c, 0, b).start()
+
+    def own_z(c):
         ag(c, 2, b, over).start()
-        cf(c, 0, b).start()
 
     s1, s2, s3, s4 = at(yd, zh, co), at(yu, zh, co), at(y, oz, co), at(yo, zh, co)
     s5, s6, s7 = at(yd, oz, co), at(yu, oz, co), at(yo, oz, co)
 
-    def early(c, ahead):
+    def ring(c):
         ag(c, 0, s1, up).wait_recv()
         ag(c, 3, s1, up, 0).start()
         cf(c, 3, s1).start()
         ag(c, 1, s2, down).wait_recv()
         ag(c, 4, s2, down, 128).start()
         cf(c, 1, s2).start()
+
+    def across(c):
         ag(c, 2, s3, over).wait_recv()
         ag(c, 5, s3, up).start()
         ag(c, 6, s3, down).start()
         cf(c, 4, s3).start()
-        ahead()
-
-    def middle(c):
+
+    def far(c):
         ag(c, 3, s4, up, 0).wait_recv()
         ag(c, 7, s4, over, 0).start()
         ag(c, 4, s4, down, 128).wait_recv()
@@ -171,34 +194,47 @@
         sb[c] = tot
         rc(sb.at[c], zb.at[c], zl_s.at[c], zl_r.at[c], (x * 2 + 1 - zl, b)).start()
 
+    mine = pl.ds(3 * co, 3)
+    theirs = pl.ds(3 * oc, 3)
+
     def t2(c):
         rc(sb.at[c], zb.at[c], zl_s.at[c], zl_r.at[c], sib).wait_recv()
-        mbuf[c, REACH, x] = sb[c] + zb[c]
-        for off in (2, -2, 1, -1):
-            k = REACH - off
-            rc(mbuf.at[c, REACH, x], mbuf.at[c, k, x], re_s.at[c, k], re_r.at[c, k],
-               (p, lax.rem(b + 16 + off, 16))).start()
+        mbuf[c, 2 + co, x] = sb[c] + zb[c]
+        src = mbuf.at[c, 2 + co, x]
+        rc(src, mbuf.at[c, co, x], re_s.at[c, 0], re_r.at[c, co], (p, lax.rem(b + 2 - co, 16))).start()
+        rc(src, mbuf.at[c, 4 + co, x], re_s.at[c, 1], re_r.at[c, co], (p, lax.rem(b + 15 - co, 16))).start()
+
+    def sx(c, d, xx, part):
+        return rc(mbuf.at[c, part, xx], mbuf.at[c, part, xx], sx_s.at[c, d], sx_r.at[c, d], sib)
 
     def t3(c):
-        for k in (0, 1, 3, 4):
-            rc(mbuf.at[c, k, x], mbuf.at[c, k, x], re_s.at[c, k], re_r.at[c, k], sib).wait_recv()
-        for d in range(1, 4):
-            rc(mbuf.at[c, :, x], mbuf.at[c, :, x], ax_s.at[c, d], ax_r.at[c, d],
-               (lax.rem(x + d, 4) * 2 + zl, b)).start()
+        for r in range(2):
+            got = mbuf.at[c, r + 4 * co, x]
+            rc(got, got, re_s.at[c, r], re_r.at[c, r], sib).wait_recv()
+        part = mbuf.at[c, mine, x]
+        for d in (2, 1, 3):
+            rc(part, part, ax_s.at[c, d], ax_r.at[c, d], (lax.rem(x + d, 4) * 2 + zl, b)).start()
+        sx(c, 0, x, mine).start()
+
+    def t3b(c):
+        for d in (1, 3, 2):
+            xx = lax.rem(x + 4 - d, 4)
+            part = mbuf.at[c, mine, xx]
+            rc(part, part, ax_s.at[c, d], ax_r.at[c, d], sib).wait_recv()
+            sx(c, d, xx, mine).start()
 
     def t4(c):
-        for d in range(1, 4):
-            xx = lax.rem(x + 4 - d, 4)
-            rc(mbuf.at[c, :, xx], mbuf.at[c, :, xx], ax_s.at[c, d], ax_r.at[c, d], sib).wait_recv()
-        for k in range(2 * REACH + 1):
+        for d in (0, 1, 3, 2):
+            sx(c, d, lax.rem(x + 4 - d, 4), theirs).wait_recv()
+        for k in range(6):
             for q in range(4):
                 mloc[k * 4 + q] = mbuf[c, k, q]
         count = cnt_ref[0]
-        first = (b - REACH) * 2
+        first = (b - co - REACH) * 2
 
         @pl.loop(0, 8)
         def _(s):
-            n = jnp.clip(ids_ref[0, s] - first, 0, 4 * REACH + 1)
+            n = jnp.clip(ids_ref[0, s] - first, 0, 11)
             keep = jnp.where(s < count, 1.0, 0.0).astype(F32)
             for i in range(2):
                 h, l = split(mloc[n * 2 + i] * keep)
@@ -213,8 +249,21 @@
             rows = pl.ds(pl.multiple_of(r * 256, 256), 256)
             dacc[rows] += (pq[:, :128] + pq[:, 128:] + q) * cbuf[c, rows]
 
-    send_own(0)
-    send_own(1)
+    def begin(c):
+        acc[...] = jnp.zeros_like(acc)
+        products(c, 0, 5)
+
+    def finish(c):
+        products(c, 5, 8)
+        t1(c)
+
+    steps = {"Y": own_y, "V": own_z, "E": ring, "Z": across, "F": far, "H": late, "P": begin, "Q": finish,
+             "1": t1b, "2": t2, "3": t3, "B": t3b, "4": t4}
+
+    own_y(0)
+    own_z(0)
+    own_y(1)
+    own_z(1)
 
     @pl.loop(0, 32)
     def _(i):
@@ -233,85 +282,51 @@
         lth[c] = h
         ltl[c] = l
 
-    early(0, lambda: send_own(2))
-
-    @pl.loop(0, 32)
-    def _(i):
-        b_copy(i).wait()
-        h, l = split(stage[i])
-        bh[i // 4, :, pl.ds(pl.multiple_of(lax.rem(i, 4) * 256, 256), 256)] = h
-        bl[i // 4, :, pl.ds(pl.multiple_of(lax.rem(i, 4) * 256, 256), 256)] = l
-
-    for c in range(CH):
-        pltpu.make_async_copy(cb_ref.at[:, pl.ds(c * 128, 128)], cbuf.at[c], cb_sem.at[c]).wait()
-    dcopy.wait()
-    dacc[...] = jnp.zeros_like(dacc)
-
-    @pl.loop(0, CH)
-    def _(c):
-        @pl.when(c < CH - 1)
-        def _():
-            def ahead():
-                @pl.when(c + 3 < CH)
-                def _():
-                    send_own(c + 3)
-
-            early(c + 1, ahead)
-
-        @pl.when(c > 0)
-        def _():
-            t1b(c - 1)
-
-        middle(c)
-        acc[...] = jnp.zeros_like(acc)
-        products(c, 0, 5)
-
-        @pl.when(c > 0)
-        def _():
-            t2(c - 1)
-
-        late(c)
-        products(c, 5, 8)
-        t1(c)
-
-        @pl.when(c > 0)
-        def _():
-            t3(c - 1)
-            t4(c - 1)
-
-    last = CH - 1
-    t1b(last)
-    t2(last)
+    def basis_split(_):
+        @pl.loop(0, 32)
+        def _(i):
+            b_copy(i).wait()
+            h, l = split(stage[i])
+            bh[i // 4, :, pl.ds(pl.multiple_of(lax.rem(i, 4) * 256, 256), 256)] = h
+            bl[i // 4, :, pl.ds(pl.multiple_of(lax.rem(i, 4) * 256, 256), 256)] = l
+
+        for c in range(CH):
+            pltpu.make_async_copy(cb_ref.at[:, pl.ds(c * 128, 128)], cbuf.at[c], cb_sem.at[c]).wait()
+        dcopy.wait()
+        dacc[...] = jnp.zeros_like(dacc)
 
     def dg(d, row):
         return rc(dpart.at[:, pl.ds(pl.multiple_of(row * 16, 16), 16)], dgb.at[d], dg_s.at[d], dg_r.at[d],
                   (p, lax.rem(b + d, 16)))
 
-    @pl.loop(1, 16)
-    def _(d):
-        dg(d, lax.rem(b + d, 16)).start()
-
-    t3(last)
-
-    dsum[...] = dpart[:, pl.ds(pl.multiple_of(b * 16, 16), 16)]
-
-    @pl.loop(1, 16)
-    def _(d):
-        dg(d, 0).wait_recv()
-        dsum[...] += dgb[d]
-
-    for c in range(CH):
-        cols = slice((c % 2) * 128, (c % 2) * 128 + 128)
-        dsum[c] = wr * dv[0, c // 2, :, cols] - wi * dv[1, c // 2, :, cols] - dsum[c]
-
     def dp(d):
         return rc(dsum, dpb.at[d], dp_s.at[d], dp_r.at[d], (lax.rem(p + d, 8), b))
 
-    @pl.loop(1, 8)
-    def _(d):
-        dp(d).start()
-
-    t4(last)
+    def diag_send(_):
+        @pl.loop(1, 16)
+        def _(d):
+            dg(d, lax.rem(b + d, 16)).start()
+
+    def diag_sum(_):
+        dsum[...] = dpart[:, pl.ds(pl.multiple_of(b * 16, 16), 16)]
+
+        @pl.loop(1, 16)
+        def _(d):
+            dg(d, 0).wait_recv()
+            dsum[...] += dgb[d]
+
+        for c in range(CH):
+            cols = slice((c % 2) * 128, (c % 2) * 128 + 128)
+            dsum[c] = wr * dv[0, c // 2, :, cols] - wi * dv[1, c // 2, :, cols] - dsum[c]
+
+        @pl.loop(1, 8)
+        def _(d):
+            dp(d).start()
+
+    steps.update({"C": basis_split, "D": diag_send, "S": diag_sum})
+
+    for ev, c in events():
+        steps[ev](c)
 
     for r in range(16):
         dens_ref[r, :] = jnp.sum(dacc[r * 128 : (r + 1) * 128].T, axis=0)
@@ -335,10 +350,12 @@
             cf(c, i, b).wait_send()
         for d in range(1, 4):
             rc(rsb.at[c, d], rsb.at[c, d], rs_s.at[c, d], rs_r.at[c, d], sib).wait_send()
-            rc(mbuf.at[c, :, x], mbuf.at[c, :, x], ax_s.at[c, d], ax_r.at[c, d], sib).wait_send()
+            rc(mbuf.at[c, mine, x], mbuf.at[c, mine, x], ax_s.at[c, d], ax_r.at[c, d], sib).wait_send()
         rc(sb.at[c], zb.at[c], zl_s.at[c], zl_r.at[c], sib).wait_send()
-        for k in (0, 1, 3, 4):
+        for k in range(2):
             rc(mbuf.at[c, k, x], mbuf.at[c, k, x], re_s.at[c, k], re_r.at[c, k], sib).wait_send()
+        for d in range(4):
+            sx(c, d, x, mine).wait_send()
 
     @pl.loop(1, 16)
     def _(d):
@@ -350,7 +367,6 @@
 
 
 def body(inverse_block, factor, diag_inverse, pole_weight, block_ids, block_count, basis, column_basis):
-    panels = factor[0].reshape(256, 2, CH, 128).transpose(2, 0, 1, 3).reshape(CH, 256, 256)
     dma = pltpu.SemaphoreType.DMA
     anyspace = pl.BlockSpec(memory_space=pl.ANY)
     smem = pl.BlockSpec(memory_space=pltpu.SMEM)
@@ -369,7 +385,7 @@
             pltpu.VMEM((8, 256, 1024), BF16),
             pltpu.VMEM((8, 256, 1024), BF16),
             pltpu.VMEM((CH, 2048, 128), F32),
-            pltpu.VMEM((CH, 5, 4, 64, 128), F32),
+            pltpu.VMEM((CH, 6, 4, 64, 128), F32),
             pltpu.VMEM((CH, 256, 128), F32),
             pltpu.VMEM((CH, 4, 64, 128), F32),
             pltpu.VMEM((CH, 64, 128), F32),
@@ -384,15 +400,15 @@
             pltpu.VMEM((CH, 256, 256), BF16),
             pltpu.VMEM((CH, 256, 256), BF16),
             pltpu.VMEM((2, 2, 16, 256), F32),
-            pltpu.VMEM((20, 64, 128), F32),
+            pltpu.VMEM((24, 64, 128), F32),
             dma((CH, 9)), dma((CH, 9)), dma((CH, 8)), dma((CH, 8)),
-            dma((CH, 4)), dma((CH, 4)), dma((CH,)), dma((CH,)), dma((CH, 5)), dma((CH, 5)), dma((CH, 4)), dma((CH, 4)),
-            dma((16,)), dma((16,)), dma((8,)), dma((8,)), dma((32,)), dma((CH + 1,)), dma((CH,)),
+            dma((CH, 4)), dma((CH, 4)), dma((CH,)), dma((CH,)), dma((CH, 2)), dma((CH, 2)), dma((CH, 4)), dma((CH, 4)), dma((CH, 4)), dma((CH, 4)),
+            dma((16,)), dma((16,)), dma((8,)), dma((8,)), dma((32,)), dma((CH, 2)), dma((1,)), dma((CH,)),
         ],
         compiler_params=pltpu.CompilerParams(
             collective_id=0, has_side_effects=True, vmem_limit_bytes=67_000_000),
     )(pole_weight, block_ids, block_count,
-      inverse_block[0], panels, diag_inverse[0], basis[0], column_basis[0])
+      inverse_block[0], factor[0], diag_inverse[0], basis[0], column_basis[0])
     return diag, dens.reshape(1, 2048)
 
 

time: 168 us -> 120 us (0.71)
  Pallas kernels: 159 us -> 114 us
  local copies, waits for them, and re-layouts: 7.28 us -> 2.67 us
    pallas_call x1, Pallas kernels: 159 us -> 114 us  [body(): pl.pallas_call(kernel, name='selinv', out_shape=(jax.ShapeDtypeStruct((2,...]
    another operation x2 -> x0, local copies, waits for them, and re-layouts: 2.78 us -> none  [body(): factor[0].reshape(256, 2, CH, 128).transpose(2, 0, 1, 3)]
    reshape x1 -> x0, local copies, waits for them, and re-layouts: 1.83 us -> none  [body(): factor[0].reshape(256, 2, CH, 128).transpose(2, 0, 1, 3)]
where the time goes in v1:
time: 120 us; the launch traced here: 118 us
  Pallas kernels  114 us (95%)
  local copies, waits for them, and re-layouts  2.67 us (2%)
  between operations  1.29 us (1%)
    pallas_call x1, Pallas kernels, body(): pl.pallas_call(kernel, name='selinv', out_shape=(jax.ShapeDtypeStruct((2,...  114 us
    unnamed x2, local copies, waits for them, and re-layouts  2.67 us

profile of v1, /device:TPU:0, one launch (start us, length us, event | category | flops | bytes accessed | tf_op | source)
XLA Modules:
  0.0 117.7 jit_solution(1794886691138434275)
XLA Ops:
  1.3 113.7 %selinv.1 = (f32[2,16,256]{2,1,0:T(8,128)}, f32[16,128]{1,0:T(8,128)}) custom-call(f32[1,2]{1,0:T(1,128)} %w_ref.1, s32[1,8]{1,0:T(1,128)} %ids_ref.1, s32[1]{0:T(128)S(6)} %copy.12.cnt_ref, f32[2,256,4096]{2,1,0:T(8,128)} %bitcast.6, f32[256,2,512]{2,1,0:T(2,128)} %bitcast.9, f32[2,2,16,256]{3,2,1,0:T(8,128)} %bitcast.10, f32[2048,1024]{1,0:T(8,128)} %bitcast.7, ...), custom_call_target="tpu_custom_call" | custom-call | tf_op jit(solution)/shard_map/selinv/pallas_call | solution.py:374
  115.0 1.4 %copy.13 = f32[2,16,256]{2,1,0:T(8,128)} copy(f32[2,16,256]{2,1,0:T(8,128)} %get-tuple-element.8) | data formatting | bytes 65536
  116.4 1.3 %copy.14 = f32[1,2048]{1,0:T(1,128)} copy(f32[1,2048]{1,0:T(1,128)} %bitcast.11) | data formatting | bytes 16384

commit v2 on v1

--- a/solution.py
+++ b/solution.py
@@ -16,10 +16,10 @@
     "E0Z0C0Y2V2E1Z1F0",
     "P0Y3H0Q0V3F1E2Z2",
     "P110H1Q1F2E3Z3P2",
-    "2011H2Q230F3P321",
-    "H3Q312B031132240",
-    "23B1D03233S041B2",
-    "42B343",
+    "2011H2Q230F3P3H3",
+    "Q31221132231B023",
+    "403233B1D041B242",
+    "B3S043",
 )
 
 
@@ -46,7 +46,7 @@
     diag_ref, dens_ref,
     lbuf, gh, gl, stage, bh, bl, cbuf, mbuf, ybuf, rsb, sb, zb, dpart, dgb, dpb, dsum,
     acc, dacc, selh, lth, ltl, dv, mloc,
-    ag_s, ag_r, co_s, co_r, rs_s, rs_r, zl_s, zl_r, re_s, re_r, ax_s, ax_r, sx_s, sx_r,
+    ag_s, ag_r, co_s, co_r, rs_s, rs_r, zl_s, zl_r, re_s, re_r, ao_s, ao_r, ax_s, ax_r, sx_s, sx_r,
     dg_s, dg_r, dp_s, dp_r, st_sem, own_sem, loc_sem, cb_sem,
 ):
     p = lax.axis_index("pole")
@@ -196,6 +196,7 @@
 
     mine = pl.ds(3 * co, 3)
     theirs = pl.ds(3 * oc, 3)
+    others = pl.ds(4 * co, 2)
 
     def t2(c):
         rc(sb.at[c], zb.at[c], zl_s.at[c], zl_r.at[c], sib).wait_recv()
@@ -203,6 +204,8 @@
         src = mbuf.at[c, 2 + co, x]
         rc(src, mbuf.at[c, co, x], re_s.at[c, 0], re_r.at[c, co], (p, lax.rem(b + 2 - co, 16))).start()
         rc(src, mbuf.at[c, 4 + co, x], re_s.at[c, 1], re_r.at[c, co], (p, lax.rem(b + 15 - co, 16))).start()
+        for d in (2, 1, 3):
+            rc(src, src, ao_s.at[c, d], ao_r.at[c, d], (lax.rem(x + d, 4) * 2 + zl, b)).start()
 
     def sx(c, d, xx, part):
         return rc(mbuf.at[c, part, xx], mbuf.at[c, part, xx], sx_s.at[c, d], sx_r.at[c, d], sib)
@@ -211,7 +214,7 @@
         for r in range(2):
             got = mbuf.at[c, r + 4 * co, x]
             rc(got, got, re_s.at[c, r], re_r.at[c, r], sib).wait_recv()
-        part = mbuf.at[c, mine, x]
+        part = mbuf.at[c, others, x]
         for d in (2, 1, 3):
             rc(part, part, ax_s.at[c, d], ax_r.at[c, d], (lax.rem(x + d, 4) * 2 + zl, b)).start()
         sx(c, 0, x, mine).start()
@@ -219,7 +222,9 @@
     def t3b(c):
         for d in (1, 3, 2):
             xx = lax.rem(x + 4 - d, 4)
-            part = mbuf.at[c, mine, xx]
+            own_block = mbuf.at[c, 2 + co, xx]
+            rc(own_block, own_block, ao_s.at[c, d], ao_r.at[c, d], sib).wait_recv()
+            part = mbuf.at[c, others, xx]
             rc(part, part, ax_s.at[c, d], ax_r.at[c, d], sib).wait_recv()
             sx(c, d, xx, mine).start()
 
@@ -242,11 +247,11 @@
                 selh[rows, :128] = h
                 selh[rows, 128:] = l
 
-        @pl.loop(0, 8)
+        @pl.loop(0, 4)
         def _(r):
             pq = dot(bh[r], selh[...])
             q = dot(bl[r], selh[:, :128])
-            rows = pl.ds(pl.multiple_of(r * 256, 256), 256)
+            rows = pl.ds(pl.multiple_of(r * 512, 512), 512)
             dacc[rows] += (pq[:, :128] + pq[:, 128:] + q) * cbuf[c, rows]
 
     def begin(c):
@@ -287,8 +292,8 @@
         def _(i):
             b_copy(i).wait()
             h, l = split(stage[i])
-            bh[i // 4, :, pl.ds(pl.multiple_of(lax.rem(i, 4) * 256, 256), 256)] = h
-            bl[i // 4, :, pl.ds(pl.multiple_of(lax.rem(i, 4) * 256, 256), 256)] = l
+            bh[i // 8, pl.ds(pl.multiple_of(lax.rem(i // 4, 2) * 256, 256), 256), pl.ds(pl.multiple_of(lax.rem(i, 4) * 256, 256), 256)] = h
+            bl[i // 8, pl.ds(pl.multiple_of(lax.rem(i // 4, 2) * 256, 256), 256), pl.ds(pl.multiple_of(lax.rem(i, 4) * 256, 256), 256)] = l
 
         for c in range(CH):
             pltpu.make_async_copy(cb_ref.at[:, pl.ds(c * 128, 128)], cbuf.at[c], cb_sem.at[c]).wait()
@@ -350,7 +355,8 @@
             cf(c, i, b).wait_send()
         for d in range(1, 4):
             rc(rsb.at[c, d], rsb.at[c, d], rs_s.at[c, d], rs_r.at[c, d], sib).wait_send()
-            rc(mbuf.at[c, mine, x], mbuf.at[c, mine, x], ax_s.at[c, d], ax_r.at[c, d], sib).wait_send()
+            rc(mbuf.at[c, others, x], mbuf.at[c, others, x], ax_s.at[c, d], ax_r.at[c, d], sib).wait_send()
+            rc(mbuf.at[c, 2 + co, x], mbuf.at[c, 2 + co, x], ao_s.at[c, d], ao_r.at[c, d], sib).wait_send()
         rc(sb.at[c], zb.at[c], zl_s.at[c], zl_r.at[c], sib).wait_send()
         for k in range(2):
             rc(mbuf.at[c, k, x], mbuf.at[c, k, x], re_s.at[c, k], re_r.at[c, k], sib).wait_send()
@@ -382,8 +388,8 @@
             pltpu.VMEM((32, 256, 256), BF16),
             pltpu.VMEM((32, 256, 256), BF16),
             pltpu.VMEM((32, 256, 256), F32),
-            pltpu.VMEM((8, 256, 1024), BF16),
-            pltpu.VMEM((8, 256, 1024), BF16),
+            pltpu.VMEM((4, 512, 1024), BF16),
+            pltpu.VMEM((4, 512, 1024), BF16),
             pltpu.VMEM((CH, 2048, 128), F32),
             pltpu.VMEM((CH, 6, 4, 64, 128), F32),
             pltpu.VMEM((CH, 256, 128), F32),
@@ -402,7 +408,7 @@
             pltpu.VMEM((2, 2, 16, 256), F32),
             pltpu.VMEM((24, 64, 128), F32),
             dma((CH, 9)), dma((CH, 9)), dma((CH, 8)), dma((CH, 8)),
-            dma((CH, 4)), dma((CH, 4)), dma((CH,)), dma((CH,)), dma((CH, 2)), dma((CH, 2)), dma((CH, 4)), dma((CH, 4)), dma((CH, 4)), dma((CH, 4)),
+            dma((CH, 4)), dma((CH, 4)), dma((CH,)), dma((CH,)), dma((CH, 2)), dma((CH, 2)), dma((CH, 4)), dma((CH, 4)), dma((CH, 4)), dma((CH, 4)), dma((CH, 4)), dma((CH, 4)),
             dma((16,)), dma((16,)), dma((8,)), dma((8,)), dma((32,)), dma((CH, 2)), dma((1,)), dma((CH,)),
         ],
         compiler_params=pltpu.CompilerParams(

time: 120 us -> 116 us (0.967)
  Pallas kernels: 114 us -> 111 us
    pallas_call x1, Pallas kernels: 114 us -> 111 us  [body(): pl.pallas_call(kernel, name='selinv', out_shape=(jax.ShapeDtypeStruct((2,...]
where the time goes in v2:
time: 116 us; the launch traced here: 115 us
  Pallas kernels  111 us (96%)
  local copies, waits for them, and re-layouts  2.67 us (2%)
  between operations  1.29 us (1%)
    pallas_call x1, Pallas kernels, body(): pl.pallas_call(kernel, name='selinv', out_shape=(jax.ShapeDtypeStruct((2,...  111 us
    unnamed x2, local copies, waits for them, and re-layouts  2.67 us

profile of v2, /device:TPU:0, one launch (start us, length us, event | category | flops | bytes accessed | tf_op | source)
XLA Modules:
  0.0 114.6 jit_solution(10462771601689496794)
XLA Ops:
  1.3 110.7 %selinv.1 = (f32[2,16,256]{2,1,0:T(8,128)}, f32[16,128]{1,0:T(8,128)}) custom-call(f32[1,2]{1,0:T(1,128)} %w_ref.1, s32[1,8]{1,0:T(1,128)} %ids_ref.1, s32[1]{0:T(128)S(6)} %copy.12.cnt_ref, f32[2,256,4096]{2,1,0:T(8,128)} %bitcast.6, f32[256,2,512]{2,1,0:T(2,128)} %bitcast.9, f32[2,2,16,256]{3,2,1,0:T(8,128)} %bitcast.10, f32[2048,1024]{1,0:T(8,128)} %bitcast.7, ...), custom_call_target="tpu_custom_call" | custom-call | tf_op jit(solution)/shard_map/selinv/pallas_call | solution.py:380
  111.9 1.4 %copy.13 = f32[2,16,256]{2,1,0:T(8,128)} copy(f32[2,16,256]{2,1,0:T(8,128)} %get-tuple-element.8) | data formatting | bytes 65536
  113.3 1.3 %copy.14 = f32[1,2048]{1,0:T(1,128)} copy(f32[1,2048]{1,0:T(1,128)} %bitcast.11) | data formatting | bytes 16384

commit v3 on v2

--- a/solution.py
+++ b/solution.py
@@ -14,8 +14,8 @@
 
 ORDER = (
     "E0Z0C0Y2V2E1Z1F0",
-    "P0Y3H0Q0V3F1E2Z2",
-    "P110H1Q1F2E3Z3P2",
+    "P0Y3H0Q0V3F1E2P1",
+    "10H1Q1E3Z2F2Z3P2",
     "2011H2Q230F3P3H3",
     "Q31221132231B023",
     "403233B1D041B242",

time: 116 us -> 121 us (1.043)
  Pallas kernels: 111 us -> 115 us
    pallas_call x1, Pallas kernels: 111 us -> 115 us  [body(): pl.pallas_call(kernel, name='selinv', out_shape=(jax.ShapeDtypeStruct((2,...]
where the time goes in v3:
time: 121 us; the launch traced here: 119 us
  Pallas kernels  115 us (95%)
  local copies, waits for them, and re-layouts  2.67 us (2%)
  between operations  1.29 us (1%)
    pallas_call x1, Pallas kernels, body(): pl.pallas_call(kernel, name='selinv', out_shape=(jax.ShapeDtypeStruct((2,...  115 us
    unnamed x2, local copies, waits for them, and re-layouts  2.67 us

profile of v3, /device:TPU:0, one launch (start us, length us, event | category | flops | bytes accessed | tf_op | source)
XLA Modules:
  0.0 118.6 jit_solution(4141525228344707647)
XLA Ops:
  1.3 114.6 %selinv.1 = (f32[2,16,256]{2,1,0:T(8,128)}, f32[16,128]{1,0:T(8,128)}) custom-call(f32[1,2]{1,0:T(1,128)} %w_ref.1, s32[1,8]{1,0:T(1,128)} %ids_ref.1, s32[1]{0:T(128)S(6)} %copy.12.cnt_ref, f32[2,256,4096]{2,1,0:T(8,128)} %bitcast.6, f32[256,2,512]{2,1,0:T(2,128)} %bitcast.9, f32[2,2,16,256]{3,2,1,0:T(8,128)} %bitcast.10, f32[2048,1024]{1,0:T(8,128)} %bitcast.7, ...), custom_call_target="tpu_custom_call" | custom-call | tf_op jit(solution)/shard_map/selinv/pallas_call | solution.py:380
  115.9 1.4 %copy.13 = f32[2,16,256]{2,1,0:T(8,128)} copy(f32[2,16,256]{2,1,0:T(8,128)} %get-tuple-element.8) | data formatting | bytes 65536
  117.3 1.3 %copy.14 = f32[1,2048]{1,0:T(1,128)} copy(f32[1,2048]{1,0:T(1,128)} %bitcast.11) | data formatting | bytes 16384
